TPU v7x, 32 devices: a whole 2x2x4 slice. The times are simulated.
32 devices in a mesh: ba: 4 (over x, core), ma: 4 (over z), row: 2 (over y).
Axes of the slice: x: 2, y: 2, z: 4, core: 2. Of those that a mesh axis runs over, the one named last changes fastest.
Arguments:
- tokens: bfloat16 [8, 256, 4096], P(('ba', 'row'), None, 'ma'), may hold values from -6 to 6
- attn_gain: bfloat16 [4096], P('ma'), may hold values from 0.25 to 1.75
- query_weight: bfloat16 [4096, 4096], P('row', 'ma'), may hold values from -0.046875 to 0.046875
- key_weight: bfloat16 [4096, 4096], P('row', 'ma'), may hold values from -0.046875 to 0.046875
- value_projection_matrix: bfloat16 [4096, 4096], P('row', 'ma'), may hold values from -0.09375 to 0.09375
- attention_output_matrix: bfloat16 [4096, 4096], P('ma', 'row'), may hold values from -0.125 to 0.125
- bucket_bias_matrix: float32 [32, 64], P(None, 'ma'), may hold values from -6 to 215, as said below
- ffn_gain: bfloat16 [4096], P('ma'), may hold values from 0.25 to 1.75
- gate_weight: bfloat16 [4096, 8192], P(None, ('ma', 'row')), may hold values from -0.09375 to 0.09375
- up_weight: bfloat16 [4096, 8192], P(None, ('ma', 'row')), may hold values from -0.09375 to 0.09375
- down_projection_weight: bfloat16 [8192, 4096], P(('ma', 'row')), may hold values from -0.09375 to 0.09375
Outputs:
- encoded: bfloat16 [8, 256, 4096], P(('ba', 'row'), None, 'ma')
Inputs may be any that keep to these rules, and one draw needn't show every extreme that they name: `bucket_bias_matrix`: entries of the relative position table.
All inputs are finite; a program needn't handle non-finite values.
Results may differ from a plain program's by a relative error of at most 0.017.
Values may be sent and summed in bfloat16 or wider, within the bound.
A program may use at most 128 MiB of HBM per device.

v0:
```python
import jax
import jax.numpy as jnp
from jax import lax
from jax.sharding import PartitionSpec as P

bucket_thresholds = (1, 2, 3, 4, 5, 6, 7, 8, 11, 16, 23, 32, 45, 64, 91, 128)
epsilon = 1e-06


def buckets(length):
    places = jnp.arange(length, dtype=jnp.int32)
    offset = places[None, :] - places[:, None]
    distance = jnp.abs(offset)
    backward = jnp.zeros_like(distance)
    for threshold in bucket_thresholds[:15]:
        backward = backward + (distance >= threshold).astype(jnp.int32)
    forward = jnp.full_like(distance, 15)
    for threshold in bucket_thresholds:
        forward = forward + (distance >= threshold).astype(jnp.int32)
    return jnp.where(offset > 0, forward, backward)


def rms_scale(values, gain):
    mean_square = jnp.mean(values * values, axis=-1, keepdims=True)
    return (values * lax.rsqrt(mean_square + epsilon) * gain.astype(jnp.float32)).astype(
        jnp.bfloat16
    )


def regroup(values, norm_gain_vector):
    widened = (
        lax.all_gather(values, "ma", axis=1, tiled=True),
        lax.all_gather(norm_gain_vector, "ma", axis=1, tiled=True),
    )
    stacked = lax.all_gather(widened[0], "row", axis=0, tiled=True)
    return (stacked, widened[1])


def on_device(
    tokens,
    attn_gain,
    query_weight,
    key_weight,
    value_projection_matrix,
    attention_output_matrix,
    bucket_bias_matrix,
    ffn_gain,
    gate_weight,
    up_weight,
    down_projection_weight,
):
    sequences, length, part_width = tokens.shape
    ma_count = lax.axis_size("ma")
    local_heads = bucket_bias_matrix.shape[1]
    inner_width = query_weight.shape[1]
    head_size = inner_width // local_heads
    slab_rows = sequences * length
    token_rows = tokens.reshape(slab_rows, part_width)
    token_float = token_rows.astype(jnp.float32)
    full_weights = (
        lax.all_gather(query_weight, "row", axis=0, tiled=True),
        lax.all_gather(key_weight, "row", axis=0, tiled=True),
        lax.all_gather(value_projection_matrix, "row", axis=0, tiled=True),
    )
    whole_rows, whole_gain = (
        lax.all_gather(token_rows, "ma", axis=1, tiled=True),
        lax.all_gather(attn_gain.reshape(1, part_width), "ma", axis=1, tiled=True),
    )
    normed = rms_scale(whole_rows.astype(jnp.float32), whole_gain[0])
    projected = tuple(
        (jnp.dot(normed, matrix, preferred_element_type=jnp.float32) for matrix in full_weights)
    )
    query_heads, key_heads, value_heads = [
        member.astype(jnp.bfloat16).reshape(sequences, length, local_heads, head_size)
        for member in projected
    ]
    bucket_grid = buckets(length)
    table_rows = jnp.arange(bucket_bias_matrix.shape[0], dtype=jnp.int32)
    bucket_indicator = (table_rows[:, None, None] == bucket_grid[None, :, :]).astype(jnp.float32)
    relative_position_scores = jnp.einsum(
        "dmy,du->umy", bucket_indicator, bucket_bias_matrix, precision=lax.Precision.HIGHEST
    )
    scores = (
        jnp.einsum("sqhd,skhd->shqk", query_heads, key_heads, preferred_element_type=jnp.float32)
        + relative_position_scores[None]
    )
    row_max = jnp.max(scores, axis=-1, keepdims=True)
    exponent = jnp.exp(scores - row_max)
    weights = (exponent / jnp.sum(exponent, axis=-1, keepdims=True)).astype(jnp.bfloat16)
    attended = jnp.einsum(
        "shqk,skhd->sqhd", weights, value_heads, preferred_element_type=jnp.float32
    )
    attended = attended.astype(jnp.bfloat16).reshape(slab_rows, inner_width)
    partial_out = jnp.dot(
        attended,
        lax.all_gather(attention_output_matrix, "row", axis=1, tiled=True),
        preferred_element_type=jnp.float32,
    )
    attn_out = lax.psum_scatter(
        partial_out.astype(jnp.bfloat16), "ma", scatter_dimension=1, tiled=True
    ).astype(jnp.float32)
    residual_stream = (token_float + attn_out).astype(jnp.bfloat16)
    residual_f = residual_stream.astype(jnp.float32)
    norm_gain_vector = ffn_gain.reshape(1, part_width)
    gate_full, up_full, down_full = (gate_weight, up_weight, down_projection_weight)
    group_rows, group_gain = regroup(residual_stream, norm_gain_vector)
    ffn_in = rms_scale(group_rows.astype(jnp.float32), group_gain[0])
    gate_act = jnp.dot(ffn_in, gate_full, preferred_element_type=jnp.float32)
    up_act = jnp.dot(ffn_in, up_full, preferred_element_type=jnp.float32)
    hidden = (jax.nn.gelu(gate_act, approximate=True) * up_act).astype(jnp.bfloat16)
    down_blocks = down_full.reshape(down_full.shape[0], ma_count, part_width)
    down_terms = jnp.einsum("tf,fmd->mtd", hidden, down_blocks, preferred_element_type=jnp.float32)
    down_terms = down_terms.reshape(ma_count * ffn_in.shape[0], part_width)
    ffn_out = lax.psum_scatter(
        down_terms.astype(jnp.bfloat16), ("ma", "row"), scatter_dimension=0, tiled=True
    ).astype(jnp.float32)
    encoded = (residual_f + ffn_out).astype(jnp.bfloat16)
    return encoded.reshape(sequences, length, part_width)


def solution(mesh):
    in_specs = (
        P(("ba", "row"), None, "ma"),
        P("ma"),
        P("row", "ma"),
        P("row", "ma"),
        P("row", "ma"),
        P("ma", "row"),
        P(None, "ma"),
        P("ma"),
        P(None, ("ma", "row")),
        P(None, ("ma", "row")),
        P(("ma", "row"), None),
    )
    out_specs = P(("ba", "row"), None, "ma")
    return jax.shard_map(
        on_device, mesh=mesh, in_specs=in_specs, out_specs=out_specs, check_vma=False
    )
```

profile of v0, /device:TPU:0, one launch (start us, length us, event | category | flops | bytes accessed | tf_op | source)
XLA Modules:
  0.0 752.7 jit_solution(16300057747724244085)
XLA Ops:
  10.0 13.7 %all-gather.1 = bf16[4096]{0:T(1024)(128)(2,1)S(1)} all-gather(bf16[1024]{0:T(1024)(128)(2,1)S(1)} %copy-done.7), channel_id=3, replica_groups=mesh['ba'=4,'ma'=4,'row'=2] {'ma'}, dimensions={0}, use_global_device_ids=true | all-gather | bytes 10240 | tf_op jit(solution)/shard_map/all_gather | solution.py:67
  24.1 4.2 fusion.7
  28.3 5.3 copy.27
  33.6 23.8 %all-gather.23.cloned.1.call-done = bf16[1,256,4096]{2,1,0:T(8,128)(2,1)} async-done(((bf16[1,256,1024]{2,1,0:T(8,128)(2,1)}), bf16[1,256,4096]{2,1,0:T(8,128)(2,1)}) %all-gather.23.cloned.1.call-update) | async-done | bytes 2097168 | tf_op jit(solution)/shard_map/all_gather | solution.py:66
  57.3 2.1 fusion.8
  59.4 102.2 %all-gather.13.cloned.1.call-done = bf16[4096,1024]{1,0:T(8,128)(2,1)} async-done(((bf16[2048,1024]{1,0:T(8,128)(2,1)}), bf16[4096,1024]{1,0:T(8,128)(2,1)}) %all-gather.13.cloned.1.call-update) | async-done | bytes 8388624 | tf_op jit(solution)/shard_map/all_gather | solution.py:61
  161.7 6.4 convolution_convert_fusion.2
  168.3 99.0 %all-gather.15.cloned.1.call-done = bf16[4096,1024]{1,0:T(8,128)(2,1)} async-done(((bf16[2048,1024]{1,0:T(8,128)(2,1)}), bf16[4096,1024]{1,0:T(8,128)(2,1)}) %all-gather.15.cloned.1.call-update) | async-done | bytes 8388624 | tf_op jit(solution)/shard_map/all_gather | solution.py:62
  267.3 6.6 convolution_convert_fusion.1
  275.2 97.5 %all-gather.11.cloned.1.call-done = bf16[4096,1024]{1,0:T(8,128)(2,1)} async-done(((bf16[2048,1024]{1,0:T(8,128)(2,1)}), bf16[4096,1024]{1,0:T(8,128)(2,1)}) %all-gather.11.cloned.1.call-update) | async-done | bytes 8388624 | tf_op jit(solution)/shard_map/all_gather | solution.py:63
  372.7 6.6 convolution_convert_fusion.3
  380.6 3.6 bitcast_add_fusion
  387.1 5.3 fusion.26
  392.3 85.8 %all-gather.17.cloned.1.call-done = bf16[1024,4096]{1,0:T(8,128)(2,1)} async-done(((bf16[1024,2048]{1,0:T(8,128)(2,1)}), bf16[1024,4096]{1,0:T(8,128)(2,1)}) %all-gather.17.cloned.1.call-update) | async-done | bytes 8388624 | tf_op jit(solution)/shard_map/all_gather | solution.py:96
  478.1 7.2 convolution_convert_fusion
  485.4 43.7 %reduce-scatter.3.cloned.1.call-done = bf16[256,1024]{1,0:T(8,128)(2,1)} async-done(((bf16[256,4096]{1,0:T(8,128)(2,1)}), bf16[256,1024]{1,0:T(8,128)(2,1)}) %reduce-scatter.3.cloned.1.call-update) | async-done | bytes 524304 | tf_op jit(solution)/shard_map/reduce_scatter | solution.py:99
  531.2 45.0 %all-gather.19.cloned.1.call-done = bf16[256,4096]{1,0:T(8,128)(2,1)} async-done(((bf16[256,1024]{1,0:T(8,128)(2,1)}), bf16[256,4096]{1,0:T(8,128)(2,1)}) %all-gather.19.cloned.1.call-update) | async-done | bytes 2097168 | tf_op jit(solution)/shard_map/all_gather | solution.py:32
  576.3 12.2 %all-gather.2 = bf16[4096]{0:T(1024)(128)(2,1)S(1)} all-gather(bf16[1024]{0:T(1024)(128)(2,1)S(1)} %copy-done.8), channel_id=4, replica_groups=mesh['ba'=4,'ma'=4,'row'=2] {'ma'}, dimensions={0}, use_global_device_ids=true | all-gather | bytes 10240 | tf_op jit(solution)/shard_map/all_gather | solution.py:33
  588.5 44.9 %all-gather.21.cloned.1.call-done = bf16[512,4096]{1,0:T(8,128)(2,1)} async-done(((bf16[256,4096]{1,0:T(8,128)(2,1)}), bf16[512,4096]{1,0:T(8,128)(2,1)}) %all-gather.21.cloned.1.call-update) | async-done | bytes 4194320 | tf_op jit(solution)/shard_map/all_gather | solution.py:35
  633.3 3.2 fusion.1
  636.8 7.7 %fusion.28 = f32[512,1024]{1,0:T(8,128)S(1)} fusion(bf16[4096,1024]{1,0:T(8,128)(2,1)} %param.19, bf16[512,4096]{1,0:T(8,128)(2,1)S(1)} %copy-done.4, f32[4096]{0:T(1024)S(1)} %mul.97, f32[512]{0:T(512)S(1)} %add_rsqrt_fusion), kind=kOutput, calls=%fused_computation.38 | convolution fusion | flops 4303355904 | bytes 14698496 | tf_op jit(solution)/shard_map/dot_general | solution.py:108
  644.6 4.9 fusion.25
  649.5 6.2 fusion.12
  655.6 88.5 %reduce-scatter.5.cloned.1.call-done = bf16[256,1024]{1,0:T(8,128)(2,1)} async-done(((bf16[2048,1024]{1,0:T(8,128)(2,1)}), bf16[256,1024]{1,0:T(8,128)(2,1)}) %reduce-scatter.5.cloned.1.call-update) | async-done | bytes 524304 | tf_op jit(solution)/shard_map/reduce_scatter | solution.py:114
  (57 shorter events, 13.9 us)
Async XLA Ops:
  6.5 17.5 %copy-start = (f32[32,16]{0,1:T(8,128)S(1)}, f32[32,16]{0,1:T(8,128)}, u32[]{:S(2)}) copy-start(f32[32,16]{0,1:T(8,128)} %param.17) | copy-start | bytes 6148
  6.5 50.8 %all-gather.23.cloned.1.call-start = ((), (), s32[]{:S(2)}) async-start(), calls=%async_computation.10 | async-start | bytes 2621440 | tf_op jit(solution)/shard_map/all_gather | solution.py:66
  7.3 154.4 %all-gather.13.cloned.1.call-start = ((), (), s32[]{:S(2)}) async-start(), calls=%async_computation.3 | async-start | bytes 12582912 | tf_op jit(solution)/shard_map/all_gather | solution.py:61
  8.0 259.3 %all-gather.15.cloned.1.call-start = ((), (), s32[]{:S(2)}) async-start(), calls=%async_computation.4 | async-start | bytes 12582912 | tf_op jit(solution)/shard_map/all_gather | solution.py:62
  8.7 1.2 copy-start.7
  8.8 363.9 %all-gather.11.cloned.1.call-start = ((), (), s32[]{:S(2)}) async-start(), calls=%async_computation.2 | async-start | bytes 12582912 | tf_op jit(solution)/shard_map/all_gather | solution.py:63
  9.3 468.8 %all-gather.17.cloned.1.call-start = ((), (), s32[]{:S(2)}) async-start(), calls=%async_computation.5 | async-start | bytes 12582912 | tf_op jit(solution)/shard_map/all_gather | solution.py:96
  9.9 519.2 %reduce-scatter.3.cloned.1.call-start = ((), (), s32[]{:S(2)}) async-start(), calls=%async_computation.6 | async-start | bytes 2621440 | tf_op jit(solution)/shard_map/reduce_scatter | solution.py:99
  59.4 207.9 %copy-start.6 = (bf16[1,256,4096]{2,1,0:T(8,128)(2,1)S(1)}, bf16[1,256,4096]{2,1,0:T(8,128)(2,1)}, u32[]{:S(2)}) copy-start(bf16[1,256,4096]{2,1,0:T(8,128)(2,1)} %all-gather.23.cloned.1.call-done) | copy-start | bytes 6291460
  384.3 2.1 copy-start.2
  478.1 51.0 %copy-start.5 = (bf16[1,256,1024]{2,1,0:T(8,128)(2,1)S(1)}, bf16[1,256,1024]{2,1,0:T(8,128)(2,1)}, u32[]{:S(2)}) copy-start(bf16[1,256,1024]{2,1,0:T(8,128)(2,1)} %param.11) | copy-start | bytes 1572868
  485.3 91.0 %copy-start.8 = (bf16[1024]{0:T(1024)(128)(2,1)S(1)}, bf16[1024]{0:T(1024)(128)(2,1)}, u32[]{:S(2)}) copy-start(bf16[1024]{0:T(1024)(128)(2,1)} %param.18) | copy-start | bytes 6148
  485.4 90.9 %all-gather.19.cloned.1.call-start = ((), (), s32[]{:S(2)}) async-start(), calls=%async_computation.7 | async-start | bytes 2621440 | tf_op jit(solution)/shard_map/all_gather | solution.py:32
  531.2 102.1 %all-gather.21.cloned.1.call-start = ((), (), s32[]{:S(2)}) async-start(), calls=%async_computation.8 | async-start | bytes 6291456 | tf_op jit(solution)/shard_map/all_gather | solution.py:35
  576.2 167.9 %reduce-scatter.5.cloned.1.call-start = ((), (), s32[]{:S(2)}) async-start(), calls=%async_computation.9 | async-start | bytes 4718592 | tf_op jit(solution)/shard_map/reduce_scatter | solution.py:114
  633.3 3.4 copy-start.4
  633.3 11.2 %slice-start = ((s8[8388608]{0:T(1024)(128)(4,1)}), s8[4194304]{0:T(1024)(128)(4,1)S(1)}, s32[]{:S(2)}) async-start(s8[8388608]{0:T(1024)(128)(4,1)} %bitcast.54), calls=%async_computation.11 | async-start | bytes 8388608
  633.3 16.1 %slice-start.2 = ((s8[8388608]{0:T(1024)(128)(4,1)}), s8[4194304]{0:T(1024)(128)(4,1)S(1)}, s32[]{:S(2)}) async-start(s8[8388608]{0:T(1024)(128)(4,1)} %bitcast.56), calls=%async_computation.13 | async-start | bytes 8388608
  636.8 7.8 %slice-start.1 = ((s8[8388608]{0:T(1024)(128)(4,1)}), s8[4194304]{0:T(1024)(128)(4,1)S(1)}, s32[]{:S(2)}) async-start(s8[8388608]{0:T(1024)(128)(4,1)} %bitcast.54), calls=%async_computation.12 | async-start | bytes 8388608
  636.8 12.7 %slice-start.3 = ((s8[8388608]{0:T(1024)(128)(4,1)}), s8[4194304]{0:T(1024)(128)(4,1)S(1)}, s32[]{:S(2)}) async-start(s8[8388608]{0:T(1024)(128)(4,1)} %bitcast.56), calls=%async_computation.14 | async-start | bytes 8388608
  649.5 96.7 %copy-start.1 = (f32[32,16]{0,1:T(8,128)S(1)}, f32[32,16]{0,1:T(8,128)}, u32[]{:S(2)}) copy-start(f32[32,16]{0,1:T(8,128)} %param.17) | copy-start | bytes 6148
  655.6 88.5 %copy-start.3 = (bf16[256,1024]{1,0:T(8,128)(2,1)S(1)}, bf16[256,1024]{1,0:T(8,128)(2,1)}, u32[]{:S(2)}) copy-start(bf16[256,1024]{1,0:T(8,128)(2,1)} %fusion.30) | copy-start | bytes 1572868
Sparse Core Ops, SparseCore 0:
  8.9 48.3 all-gather.22
  58.9 102.7 all-gather.12
  163.2 104.0 all-gather.14
  268.7 103.9 all-gather.10
  374.1 103.9 all-gather.16
  485.5 43.6 reduce-scatter.2
  531.3 44.8 all-gather.18
  577.8 55.5 all-gather.20
  655.8 88.3 reduce-scatter.4
where the time goes:
time: 753 us
  waiting for transfers between devices  634 us (84%)
  matrix products  58.6 us (8%)
  blocking collectives  25.9 us (3%)
  between operations  13.4 us (2%)
  other arithmetic  10.5 us (1%)
  local copies, waits for them, and re-layouts  10.4 us (1%)
    all_gather x1, waiting for transfers between devices, on_device(): lax.all_gather(query_weight, 'row', axis=0, tiled=True)  102 us
    all_gather x1, waiting for transfers between devices, on_device(): lax.all_gather(key_weight, 'row', axis=0, tiled=True)  99 us
    all_gather x1, waiting for transfers between devices, on_device(): lax.all_gather(value_projection_matrix, 'row', axis=0, tiled=True)  97.5 us
    reduce_scatter x1, waiting for transfers between devices, on_device(): lax.psum_scatter(down_terms.astype(jnp.bfloat16), ('ma', 'row'), scatter_...  88.5 us
    all_gather x1, waiting for transfers between devices, on_device(): lax.all_gather(attention_output_matrix, 'row', axis=1, tiled=True)  85.8 us
    all_gather x1, waiting for transfers between devices, regroup(): lax.all_gather(values, 'ma', axis=1, tiled=True)  45 us
    all_gather x1, waiting for transfers between devices, regroup(): stacked = lax.all_gather(widened[0], 'row', axis=0, tiled=True)  44.9 us
    reduce_scatter x1, waiting for transfers between devices, on_device(): lax.psum_scatter(partial_out.astype(jnp.bfloat16), 'ma', scatter_dimensio...  43.7 us
  transfers between devices with their start and end apart: 9, of which 9 were waited for; matrix products, arithmetic and copies ran while one was open for 6% of the time, Pallas kernels for 0%

commit v1 on v0

--- a/solution.py
+++ b/solution.py
@@ -5,6 +5,18 @@
 
 bucket_thresholds = (1, 2, 3, 4, 5, 6, 7, 8, 11, 16, 23, 32, 45, 64, 91, 128)
 epsilon = 1e-06
+
+
+def doubled_up(shard, axis, dim):
+    ways, here = (lax.axis_size(axis), lax.axis_index(axis))
+    grown, reach = (shard, 1)
+    while reach < ways:
+        theirs = lax.ppermute(grown, axis, [(d, d ^ reach) for d in range(ways)])
+        mine_first = jnp.concatenate([grown, theirs], axis=dim)
+        theirs_first = jnp.concatenate([theirs, grown], axis=dim)
+        grown = jnp.where(here & reach == 0, mine_first, theirs_first)
+        reach = 2 * reach
+    return grown
 
 
 def buckets(length):
@@ -92,9 +104,7 @@
     )
     attended = attended.astype(jnp.bfloat16).reshape(slab_rows, inner_width)
     partial_out = jnp.dot(
-        attended,
-        lax.all_gather(attention_output_matrix, "row", axis=1, tiled=True),
-        preferred_element_type=jnp.float32,
+        attended, doubled_up(attention_output_matrix, "row", 1), preferred_element_type=jnp.float32
     )
     attn_out = lax.psum_scatter(
         partial_out.astype(jnp.bfloat16), "ma", scatter_dimension=1, tiled=True

time: 753 us -> 704 us (0.935)
  waiting for transfers between devices: 634 us -> 580 us
    all_gather x1 -> x0, waiting for transfers between devices: 85.8 us -> none  [on_device(): lax.all_gather(attention_output_matrix, 'row', axis=1, tiled=True)]
    all_gather x1, waiting for transfers between devices: 102 us -> 134 us  [on_device(): lax.all_gather(query_weight, 'row', axis=0, tiled=True)]
  transfers between devices with their start and end apart: 9 -> 9, of which waited for: 9 -> 8; matrix products, arithmetic and copies ran while one was open for 6% -> 6% of each run, Pallas kernels for 0% -> 0%
where the time goes in v1:
time: 704 us; the launch traced here: 703 us
  waiting for transfers between devices  580 us (82%)
  matrix products  61.9 us (9%)
  blocking collectives  24.2 us (3%)
  between operations  13.7 us (2%)
  other arithmetic  10.5 us (1%)
  local copies, waits for them, and re-layouts  10.2 us (1%)
    all_gather x1, waiting for transfers between devices, on_device(): lax.all_gather(query_weight, 'row', axis=0, tiled=True)  134 us
    all_gather x1, waiting for transfers between devices, on_device(): lax.all_gather(key_weight, 'row', axis=0, tiled=True)  100 us
    all_gather x1, waiting for transfers between devices, on_device(): lax.all_gather(value_projection_matrix, 'row', axis=0, tiled=True)  97.5 us
    reduce_scatter x1, waiting for transfers between devices, on_device(): lax.psum_scatter(down_terms.astype(jnp.bfloat16), ('ma', 'row'), scatter_...  88.5 us
    all_gather x1, waiting for transfers between devices, regroup(): stacked = lax.all_gather(widened[0], 'row', axis=0, tiled=True)  45.1 us
    all_gather x1, waiting for transfers between devices, regroup(): lax.all_gather(values, 'ma', axis=1, tiled=True)  45 us
    reduce_scatter x1, waiting for transfers between devices, on_device(): lax.psum_scatter(partial_out.astype(jnp.bfloat16), 'ma', scatter_dimensio...  43.7 us
    all_gather x1, waiting for transfers between devices, on_device(): lax.all_gather(token_rows, 'ma', axis=1, tiled=True)  22.9 us
  transfers between devices with their start and end apart: 9, of which 8 were waited for; matrix products, arithmetic and copies ran while one was open for 6% of the time, Pallas kernels for 0%

profile of v1, /device:TPU:0, one launch (start us, length us, event | category | flops | bytes accessed | tf_op | source)
XLA Modules:
  0.0 703.4 jit_solution(3059858825615201934)
XLA Ops:
  9.4 3.1 collective-permute-start
  12.4 12.3 %all-gather.1 = bf16[4096]{0:T(1024)(128)(2,1)S(1)} all-gather(bf16[1024]{0:T(1024)(128)(2,1)S(1)} %copy-done.7), channel_id=3, replica_groups=mesh['ba'=4,'ma'=4,'row'=2] {'ma'}, dimensions={0}, use_global_device_ids=true | all-gather | bytes 10240 | tf_op jit(solution)/shard_map/all_gather | solution.py:79
  25.1 4.1 fusion.13
  29.2 5.2 copy.27
  34.4 22.9 %all-gather.20.cloned.1.call-done = bf16[1,256,4096]{2,1,0:T(8,128)(2,1)} async-done(((bf16[1,256,1024]{2,1,0:T(8,128)(2,1)}), bf16[1,256,4096]{2,1,0:T(8,128)(2,1)}) %all-gather.20.cloned.1.call-update) | async-done | bytes 2097168 | tf_op jit(solution)/shard_map/all_gather | solution.py:78
  57.3 2.1 fusion.16
  59.4 133.9 %all-gather.12.cloned.1.call-done = bf16[4096,1024]{1,0:T(8,128)(2,1)} async-done(((bf16[2048,1024]{1,0:T(8,128)(2,1)}), bf16[4096,1024]{1,0:T(8,128)(2,1)}) %all-gather.12.cloned.1.call-update) | async-done | bytes 8388624 | tf_op jit(solution)/shard_map/all_gather | solution.py:73
  193.4 6.4 convolution_convert_fusion.1
  200.0 100.4 %all-gather.14.cloned.1.call-done = bf16[4096,1024]{1,0:T(8,128)(2,1)} async-done(((bf16[2048,1024]{1,0:T(8,128)(2,1)}), bf16[4096,1024]{1,0:T(8,128)(2,1)}) %all-gather.14.cloned.1.call-update) | async-done | bytes 8388624 | tf_op jit(solution)/shard_map/all_gather | solution.py:74
  300.4 6.6 convolution_convert_fusion
  308.3 97.5 %all-gather.10.cloned.1.call-done = bf16[4096,1024]{1,0:T(8,128)(2,1)} async-done(((bf16[2048,1024]{1,0:T(8,128)(2,1)}), bf16[4096,1024]{1,0:T(8,128)(2,1)}) %all-gather.10.cloned.1.call-update) | async-done | bytes 8388624 | tf_op jit(solution)/shard_map/all_gather | solution.py:75
  405.8 6.6 convolution_convert_fusion.2
  413.6 3.0 bitcast_add_fusion
  419.3 4.5 fusion.34
  423.9 11.9 %fusion.15 = bf16[256,4096]{1,0:T(8,128)(2,1)} fusion(bf16[256,1024]{0,1:T(8,128)(2,1)S(1)} %bitcast.57, bf16[1024,2048]{1,0:T(8,128)(2,1)} %collective-permute-done, bf16[1024,2048]{1,0:T(8,128)(2,1)} %param.16, pred[]{:T(512)S(6)} %eq.19), kind=kOutput, calls=%fused_computation.21 | convolution fusion | flops 2186280960 | bytes 11010049 | tf_op jit(solution)/shard_map/dot_general | solution.py:106
  435.8 43.7 %reduce-scatter.3.cloned.1.call-done = bf16[256,1024]{1,0:T(8,128)(2,1)} async-done(((bf16[256,4096]{1,0:T(8,128)(2,1)}), bf16[256,1024]{1,0:T(8,128)(2,1)}) %reduce-scatter.3.cloned.1.call-update) | async-done | bytes 524304 | tf_op jit(solution)/shard_map/reduce_scatter | solution.py:109
  481.6 45.0 %all-gather.16.cloned.1.call-done = bf16[256,4096]{1,0:T(8,128)(2,1)} async-done(((bf16[256,1024]{1,0:T(8,128)(2,1)}), bf16[256,4096]{1,0:T(8,128)(2,1)}) %all-gather.16.cloned.1.call-update) | async-done | bytes 2097168 | tf_op jit(solution)/shard_map/all_gather | solution.py:44
  526.7 11.9 %all-gather.2 = bf16[4096]{0:T(1024)(128)(2,1)S(1)} all-gather(bf16[1024]{0:T(1024)(128)(2,1)S(1)} %copy-done.8), channel_id=4, replica_groups=mesh['ba'=4,'ma'=4,'row'=2] {'ma'}, dimensions={0}, use_global_device_ids=true | all-gather | bytes 10240 | tf_op jit(solution)/shard_map/all_gather | solution.py:45
  538.6 45.1 %all-gather.18.cloned.1.call-done = bf16[512,4096]{1,0:T(8,128)(2,1)} async-done(((bf16[256,4096]{1,0:T(8,128)(2,1)}), bf16[512,4096]{1,0:T(8,128)(2,1)}) %all-gather.18.cloned.1.call-update) | async-done | bytes 4194320 | tf_op jit(solution)/shard_map/all_gather | solution.py:47
  583.7 3.2 fusion.1
  587.2 7.7 %fusion.36 = f32[512,1024]{1,0:T(8,128)S(1)} fusion(bf16[4096,1024]{1,0:T(8,128)(2,1)} %param.19, bf16[512,4096]{1,0:T(8,128)(2,1)S(1)} %copy-done.4, f32[4096]{0:T(1024)S(1)} %mul.97, f32[512]{0:T(512)S(1)} %add_rsqrt_fusion), kind=kOutput, calls=%fused_computation.46 | convolution fusion | flops 4303355904 | bytes 14698496 | tf_op jit(solution)/shard_map/dot_general | solution.py:118
  595.0 4.9 fusion.33
  599.9 6.1 fusion.20
  606.1 88.5 %reduce-scatter.5.cloned.1.call-done = bf16[256,1024]{1,0:T(8,128)(2,1)} async-done(((bf16[2048,1024]{1,0:T(8,128)(2,1)}), bf16[256,1024]{1,0:T(8,128)(2,1)}) %reduce-scatter.5.cloned.1.call-update) | async-done | bytes 524304 | tf_op jit(solution)/shard_map/reduce_scatter | solution.py:124
  (56 shorter events, 13.1 us)
Async XLA Ops:
  6.5 18.5 %copy-start = (f32[32,16]{0,1:T(8,128)S(1)}, f32[32,16]{0,1:T(8,128)}, u32[]{:S(2)}) copy-start(f32[32,16]{0,1:T(8,128)} %param.17) | copy-start | bytes 6148
  6.5 50.8 %all-gather.20.cloned.1.call-start = ((), (), s32[]{:S(2)}) async-start(), calls=%async_computation.9 | async-start | bytes 2621440 | tf_op jit(solution)/shard_map/all_gather | solution.py:78
  7.3 186.1 %all-gather.12.cloned.1.call-start = ((), (), s32[]{:S(2)}) async-start(), calls=%async_computation.3 | async-start | bytes 12582912 | tf_op jit(solution)/shard_map/all_gather | solution.py:73
  8.0 4.4 copy-start.7
  8.0 292.4 %all-gather.14.cloned.1.call-start = ((), (), s32[]{:S(2)}) async-start(), calls=%async_computation.4 | async-start | bytes 12582912 | tf_op jit(solution)/shard_map/all_gather | solution.py:74
  8.8 397.0 %all-gather.10.cloned.1.call-start = ((), (), s32[]{:S(2)}) async-start(), calls=%async_computation.2 | async-start | bytes 12582912 | tf_op jit(solution)/shard_map/all_gather | solution.py:75
  9.3 470.2 %reduce-scatter.3.cloned.1.call-start = ((), (), s32[]{:S(2)}) async-start(), calls=%async_computation.5 | async-start | bytes 2621440 | tf_op jit(solution)/shard_map/reduce_scatter | solution.py:109
  9.4 414.5 %collective-permute-start = (bf16[1024,2048]{1,0:T(8,128)(2,1)}, bf16[1024,2048]{1,0:T(8,128)(2,1)}, u32[]{:S(2)}, u32[]{:S(2)}) collective-permute-start(bf16[1024,2048]{1,0:T(8,128)(2,1)} %param.16), channel_id=1, source_target_pairs={{0,1},{1,0},{2,3},{3,2},{4,5},{5,4},{6,7},{7,6},{8,9},{9,8},{10,11... | collective-permute-start | bytes 12582920 | tf_op jit(solution)/shard_map/ppermute | solution.py:14
  59.4 241.0 %copy-start.6 = (bf16[1,256,4096]{2,1,0:T(8,128)(2,1)S(1)}, bf16[1,256,4096]{2,1,0:T(8,128)(2,1)}, u32[]{:S(2)}) copy-start(bf16[1,256,4096]{2,1,0:T(8,128)(2,1)} %all-gather.20.cloned.1.call-done) | copy-start | bytes 6291460
  416.6 1.9 copy-start.2
  423.8 55.7 %copy-start.5 = (bf16[1,256,1024]{2,1,0:T(8,128)(2,1)S(1)}, bf16[1,256,1024]{2,1,0:T(8,128)(2,1)}, u32[]{:S(2)}) copy-start(bf16[1,256,1024]{2,1,0:T(8,128)(2,1)} %param.11) | copy-start | bytes 1572868
  435.7 91.0 %copy-start.8 = (bf16[1024]{0:T(1024)(128)(2,1)S(1)}, bf16[1024]{0:T(1024)(128)(2,1)}, u32[]{:S(2)}) copy-start(bf16[1024]{0:T(1024)(128)(2,1)} %param.18) | copy-start | bytes 6148
  435.8 90.9 %all-gather.16.cloned.1.call-start = ((), (), s32[]{:S(2)}) async-start(), calls=%async_computation.6 | async-start | bytes 2621440 | tf_op jit(solution)/shard_map/all_gather | solution.py:44
  481.6 102.1 %all-gather.18.cloned.1.call-start = ((), (), s32[]{:S(2)}) async-start(), calls=%async_computation.7 | async-start | bytes 6291456 | tf_op jit(solution)/shard_map/all_gather | solution.py:47
  526.6 167.9 %reduce-scatter.5.cloned.1.call-start = ((), (), s32[]{:S(2)}) async-start(), calls=%async_computation.8 | async-start | bytes 4718592 | tf_op jit(solution)/shard_map/reduce_scatter | solution.py:124
  583.7 3.4 copy-start.4
  583.7 11.2 %slice-start = ((s8[8388608]{0:T(1024)(128)(4,1)}), s8[4194304]{0:T(1024)(128)(4,1)S(1)}, s32[]{:S(2)}) async-start(s8[8388608]{0:T(1024)(128)(4,1)} %bitcast.52), calls=%async_computation.10 | async-start | bytes 8388608
  583.7 16.1 %slice-start.2 = ((s8[8388608]{0:T(1024)(128)(4,1)}), s8[4194304]{0:T(1024)(128)(4,1)S(1)}, s32[]{:S(2)}) async-start(s8[8388608]{0:T(1024)(128)(4,1)} %bitcast.54), calls=%async_computation.12 | async-start | bytes 8388608
  587.2 7.8 %slice-start.1 = ((s8[8388608]{0:T(1024)(128)(4,1)}), s8[4194304]{0:T(1024)(128)(4,1)S(1)}, s32[]{:S(2)}) async-start(s8[8388608]{0:T(1024)(128)(4,1)} %bitcast.52), calls=%async_computation.11 | async-start | bytes 8388608
  587.2 12.7 %slice-start.3 = ((s8[8388608]{0:T(1024)(128)(4,1)}), s8[4194304]{0:T(1024)(128)(4,1)S(1)}, s32[]{:S(2)}) async-start(s8[8388608]{0:T(1024)(128)(4,1)} %bitcast.54), calls=%async_computation.13 | async-start | bytes 8388608
  599.9 96.7 %copy-start.1 = (f32[32,16]{0,1:T(8,128)S(1)}, f32[32,16]{0,1:T(8,128)}, u32[]{:S(2)}) copy-start(f32[32,16]{0,1:T(8,128)} %param.17) | copy-start | bytes 6148
  606.0 88.5 %copy-start.3 = (bf16[256,1024]{1,0:T(8,128)(2,1)S(1)}, bf16[256,1024]{1,0:T(8,128)(2,1)}, u32[]{:S(2)}) copy-start(bf16[256,1024]{1,0:T(8,128)(2,1)} %fusion.38) | copy-start | bytes 1572868
Sparse Core Ops, SparseCore 0:
  8.9 48.3 all-gather.19
  58.9 134.4 all-gather.11
  194.9 105.4 all-gather.13
  301.8 103.9 all-gather.9
  435.9 43.5 reduce-scatter.2
  481.7 44.8 all-gather.15
  528.2 55.5 all-gather.17
  606.2 88.2 reduce-scatter.4
